TPU v7x, 32 devices: a whole 2x2x4 slice. The times are simulated.
32 devices in a mesh: gx: 8 (over y, x, core), gy: 4 (over z).
Axes of the slice: x: 2, y: 2, z: 4, core: 2. Of those that a mesh axis runs over, the one named last changes fastest.
Arguments:
- basis: float32 [32, 128, 64, 256], P(None, 'gx', 'gy'), may hold values from -0.09375 to 0.09375
- reaction: float32 [128, 64, 256], P('gx', 'gy'), may hold values from 0.5 to 4
Outputs:
- extended: float32 [32, 128, 64, 256], P(None, 'gx', 'gy')
- coarse: float32 [32, 5, 32, 32], replicated
All inputs are finite; a program needn't handle non-finite values.
Results may differ from a plain program's by a relative error of at most 0.000071.
Values sent between devices are 32-bit elements; how exact they have to be, the bound alone decides.
A program may use at most 128 MiB of HBM per device.

v0:
```python
import jax
import jax.numpy as jnp
from jax import lax
from jax.sharding import PartitionSpec as P

SWEEPS = 4


OMEGA = 0.8


def passed_along(block, axis, distance):
    devices = range(lax.axis_size(axis))
    route = [(i - distance, i) for i in devices if i - distance in devices]
    return lax.ppermute(block, axis, route)


def stencil(field, coef):
    padded = jnp.pad(field, ((0, 0), (1, 1), (1, 1), (1, 1)))
    beside = padded[:, 2:, 1:-1, 1:-1] + padded[:, :-2, 1:-1, 1:-1]
    beside = beside + padded[:, 1:-1, 2:, 1:-1] + padded[:, 1:-1, :-2, 1:-1]
    beside = beside + padded[:, 1:-1, 1:-1, 2:] + padded[:, 1:-1, 1:-1, :-2]
    return (6.0 + coef) * field - beside


def couple(own, other):
    width = own.shape[0]
    return -jnp.dot(
        own.reshape(width, -1),
        other.reshape(width, -1).T,
        precision=lax.Precision.HIGHEST,
        preferred_element_type=jnp.float32,
    )


def on_device(basis, reaction):
    width, cx, cy, cz = basis.shape
    right_face = passed_along(basis[:, 0], "gx", -1)
    upper_face = passed_along(basis[:, :, 0], "gy", -1)
    xpos = lax.broadcasted_iota(jnp.int32, (cx, cy, cz), 0)
    ypos = lax.broadcasted_iota(jnp.int32, (cx, cy, cz), 1)
    inner = (xpos >= 1) & (xpos <= cx - 2) & (ypos >= 1) & (ypos <= cy - 2)
    phi = basis
    for sweep in range(SWEEPS):
        update = OMEGA * stencil(phi, reaction) / (6.0 + reaction)
        phi = phi - jnp.where(inner[None], update, jnp.float32(0.0))
    applied = stencil(phi, reaction)
    diag = jnp.dot(
        phi.reshape(width, -1),
        applied.reshape(width, -1).T,
        precision=lax.Precision.HIGHEST,
        preferred_element_type=jnp.float32,
    )
    blocks = jnp.stack(
        [diag, couple(basis[:, -1], right_face), couple(basis[:, :, -1], upper_face)]
    )
    gathered = lax.all_gather(blocks[None], ("gx", "gy"), axis=0, tiled=True)
    columns = lax.axis_size("gy")
    plus_x = gathered[:, 1]
    plus_y = gathered[:, 2]
    minus_x = jnp.concatenate(
        [jnp.zeros((columns, width, width), jnp.float32), jnp.swapaxes(plus_x[:-columns], 1, 2)],
        axis=0,
    )
    minus_y = jnp.concatenate(
        [jnp.zeros((1, width, width), jnp.float32), jnp.swapaxes(plus_y[:-1], 1, 2)], axis=0
    )
    coarse = jnp.stack([gathered[:, 0], minus_x, plus_x, minus_y, plus_y], axis=1)
    return (phi, coarse)


def solution(mesh):
    placed = (P(None, "gx", "gy", None), P("gx", "gy", None))
    return jax.shard_map(
        on_device,
        mesh=mesh,
        in_specs=placed,
        out_specs=(P(None, "gx", "gy", None), P()),
        check_vma=False,
    )
```

profile of v0, /device:TPU:0, one launch (start us, length us, event | category | flops | bytes accessed | tf_op | source)
XLA Modules:
  0.0 207.6 jit_solution(5579963518634008711)
XLA Ops:
  0.6 5.3 %fusion.49 = (f32[32,16,1,256]{3,2,1,0:T(1,128)S(1)}, f32[32,16,256]{2,1,0:T(8,128)S(1)}) fusion(f32[32,16,16,256]{3,2,1,0:T(8,128)} %param.2), kind=kLoop, calls=%fused_computation.98 | loop fusion | bytes 2097152 | tf_op jit(solution)/shard_map/slice | solution.py:39
  6.0 1.3 collective-permute-start.1
  7.3 2.1 slice_bitcast_fusion
  9.3 1.3 collective-permute-start
  10.6 1.0 broadcast_add_fusion
  11.6 0.1 and_and_fusion
  11.7 23.6 %select_subtract_fusion.3 = f32[32,16,16,256]{3,2,1,0:T(8,128)} fusion(f32[32,16,16,256]{3,2,1,0:T(8,128)} %param.2, f32[16,16,256]{2,1,0:T(8,128)S(1)} %broadcast_add_fusion, pred[16,16,256]{2,1,0:T(8,128)(4,1)S(1)} %and_and_fusion), kind=kLoop, calls=%fused_computation.74 | loop fusion | flops 23068672 | bytes 17104896 | tf_op jit(solution)/shard_map/sub | solution.py:46
  35.4 21.9 %select_subtract_fusion.2 = f32[32,16,16,256]{3,2,1,0:T(8,128)S(1)} fusion(f32[32,16,16,256]{3,2,1,0:T(8,128)} %select_subtract_fusion.3, f32[16,16,256]{2,1,0:T(8,128)S(1)} %broadcast_add_fusion, pred[16,16,256]{2,1,0:T(8,128)(4,1)S(1)} %and_and_fusion), kind=kLoop, calls=%fused_computation.73 | loop fusion | flops 23068672 | bytes 17104896 | tf_op jit(solution)/shard_map/sub | solution.py:46
  57.3 9.6 %select_subtract_fusion.1 = f32[32,16,16,256]{3,2,1,0:T(8,128)} fusion(f32[32,16,16,256]{3,2,1,0:T(8,128)S(1)} %select_subtract_fusion.2, f32[16,16,256]{2,1,0:T(8,128)S(1)} %broadcast_add_fusion, pred[16,16,256]{2,1,0:T(8,128)(4,1)S(1)} %and_and_fusion), kind=kLoop, calls=%fused_computation.72 | loop fusion | flops 23068672 | bytes 17104896 | tf_op jit(solution)/shard_map/sub | solution.py:46
  66.9 21.9 %select_subtract_fusion = f32[32,16,16,256]{3,2,1,0:T(8,128)S(1)} fusion(f32[32,16,16,256]{3,2,1,0:T(8,128)} %select_subtract_fusion.1, f32[16,16,256]{2,1,0:T(8,128)S(1)} %broadcast_add_fusion, pred[16,16,256]{2,1,0:T(8,128)(4,1)S(1)} %and_and_fusion), kind=kLoop, calls=%fused_computation.71 | loop fusion | flops 23068672 | bytes 17104896 | tf_op jit(solution)/shard_map/sub | solution.py:46
  88.8 0.0 copy-start
  88.8 9.2 %fusion.37 = f32[32,16,16,256]{3,2,1,0:T(8,128)} fusion(f32[32,16,16,256]{3,2,1,0:T(8,128)S(1)} %select_subtract_fusion, f32[16,16,256]{2,1,0:T(8,128)S(1)} %broadcast_add_fusion), kind=kLoop, calls=%fused_computation.67 | loop fusion | flops 14680064 | bytes 17039360 | tf_op jit(solution)/shard_map/sub | solution.py:23
  98.0 0.3 copy.22
  98.3 0.3 copy.20
  98.6 0.0 copy-done
  98.6 16.0 %fusion.43 = f32[1,32,32]{2,1,0:T(8,128)S(1)} fusion(f32[32,16,16,256]{3,2,1,0:T(8,128)} %fusion.37, f32[32,16,16,256]{3,2,1,0:T(8,128)S(1)} %select_subtract_fusion), kind=kOutput, calls=%fused_computation.79 | convolution fusion | flops 805306368 | bytes 16781312 | tf_op jit(solution)/shard_map/dot_general | solution.py:48
  114.7 0.0 collective-permute-done.1
  114.7 0.3 copy.23
  115.0 0.0 collective-permute-done
  115.0 0.3 copy.21
  115.3 0.6 fusion.41
  115.9 0.6 fusion.42
  116.5 86.4 %all-gather = f32[96,32,32]{2,1,0:T(8,128)S(1)} all-gather(f32[3,32,32]{2,1,0:T(8,128)S(1)} %pad_maximum_fusion), channel_id=2, replica_groups=mesh['gx'=8,'gy'=4] {'gx','gy'}, dimensions={0}, use_global_device_ids=true | all-gather | bytes 405504 | tf_op jit(solution)/shard_map/all_gather | solution.py:57
  202.9 0.8 slice_dynamic-update-slice_fusion.2
  203.8 0.2 copy.16
  204.0 0.8 constant_dynamic-update-slice_fusion.1
  204.9 0.8 slice_dynamic-update-slice_fusion.1
  205.7 0.2 copy.17
  205.9 0.8 constant_dynamic-update-slice_fusion
  206.8 0.8 slice_dynamic-update-slice_fusion
  (8 shorter events, 0.2 us)
Async XLA Ops:
  6.0 108.7 %collective-permute-start.1 = (f32[32,16,256]{2,1,0:T(8,128)S(1)}, f32[32,16,256]{2,1,0:T(8,128)S(1)}, u32[]{:S(2)}, u32[]{:S(2)}) collective-permute-start(f32[32,16,256]{2,1,0:T(8,128)S(1)} %bitcast.52), channel_id=1, source_target_pairs={{1,0},{2,1},{3,2},{5,4},{6,5},{7,6},{9,8},{10,9},{11,10},{13,12},{... | collective-permute-start | bytes 1572872 | tf_op jit(solution)/shard_map/ppermute | solution.py:15
  9.3 105.7 %collective-permute-start = (f32[32,16,256]{2,1,0:T(8,128)}, f32[32,16,256]{2,1,0:T(8,128)S(1)}, u32[]{:S(2)}, u32[]{:S(2)}) collective-permute-start(f32[32,16,256]{2,1,0:T(8,128)} %get-tuple-element.2), channel_id=1, source_target_pairs={{4,0},{8,4},{12,8},{16,12},{20,16},{24,20},{28,24},{5,1},{9,5},{13... | collective-permute-start | bytes 1572872 | tf_op jit(solution)/shard_map/ppermute | solution.py:15
  88.8 9.9 %copy-start = (f32[32,16,16,256]{3,2,1,0:T(8,128)}, f32[32,16,16,256]{3,2,1,0:T(8,128)S(1)}, u32[]{:S(2)}) copy-start(f32[32,16,16,256]{3,2,1,0:T(8,128)S(1)} %select_subtract_fusion) | copy-start | bytes 25165828
where the time goes:
time: 208 us
  other arithmetic  87.4 us (42%)
  blocking collectives  86.4 us (42%)
  matrix products  17.1 us (8%)
  local copies, waits for them, and re-layouts  13.3 us (6%)
  starting transfers between devices  2.57 us (1%)
    all_gather x1, blocking collectives, on_device(): gathered = lax.all_gather(blocks[None], ('gx', 'gy'), axis=0, tiled=True)  86.4 us
    sub x4, other arithmetic, on_device(): phi = phi - jnp.where(inner[None], update, jnp.float32(0.0))  77 us
    dot_general x1, matrix products, on_device(): jnp.dot(phi.reshape(width, -1), applied.reshape(width, -1).T, precision=l...  16 us
    sub x1, other arithmetic, stencil(): return (6.0 + coef) * field - beside  9.23 us
    slice x1, local copies, waits for them, and re-layouts, on_device(): upper_face = passed_along(basis[:, :, 0], 'gy', -1)  5.27 us
    unnamed x11, local copies, waits for them, and re-layouts  4.6 us
  transfers between devices with their start and end apart: 2, of which 0 were waited for; matrix products, arithmetic and copies ran while one was open for 51% of the time, Pallas kernels for 0%

commit v1 on v0

v1 whole, which is shorter than its diff:
```python
import functools

import jax
import jax.numpy as jnp
from jax import lax
from jax.experimental import pallas as pl
from jax.experimental.pallas import tpu as pltpu
from jax.sharding import PartitionSpec as P

SWEEPS = 4
OMEGA = 0.8
GROUP = 8
LANES = 128


def passed_along(block, axis, distance):
    devices = range(lax.axis_size(axis))
    route = [(i - distance, i) for i in devices if i - distance in devices]
    return lax.ppermute(block, axis, route)


def along_z(field, lane):
    zero = jnp.zeros_like(field[0])
    back = [pltpu.roll(piece, 1, 1) for piece in field]
    ahead = [pltpu.roll(piece, LANES - 1, 1) for piece in field]
    sums = []
    for h in range(len(field)):
        below = jnp.where(lane == 0, back[h - 1] if h else zero, back[h])
        above = jnp.where(lane == LANES - 1, ahead[h + 1] if h + 1 < len(field) else zero, ahead[h])
        sums.append(below + above)
    return sums


def pieces(ref, x, y):
    parts = ref.shape[-1] // LANES
    return [ref[x, y, :, h * LANES:(h + 1) * LANES] for h in range(parts)]


def halves(value):
    high = value.astype(jnp.bfloat16).astype(jnp.float32)
    return jnp.concatenate([value, value - high], axis=0).astype(jnp.bfloat16)


def extend_kernel(basis, reaction, extended, product, first, second, weight, centre, left, right):
    _, cx, cy, cz = basis.shape
    parts = cz // LANES
    group = pl.program_id(0)
    lane = lax.broadcasted_iota(jnp.int32, (GROUP, LANES), 1)

    @pl.when(group == 0)
    def _():
        blank = jnp.zeros((cy, GROUP, cz), jnp.float32)
        for buffer in (first,):
            buffer[0] = blank
            buffer[cx + 1] = blank

        @pl.loop(0, cx)
        def _(x):
            whole = 6.0 + reaction[x]
            scaled = OMEGA / whole
            for y in range(cy):
                centre[x, y] = jnp.broadcast_to(whole[y:y + 1], (GROUP, cz))
                weight[x, y] = jnp.broadcast_to(scaled[y:y + 1], (GROUP, cz))

    @pl.loop(0, cx)
    def _(x):
        for y in range(0, cy, GROUP):
            turned = jnp.swapaxes(basis[:, x, y:y + GROUP, :], 0, 1)
            first[x + 1, y:y + GROUP] = turned
            if y == 0:
                second[x + 1, 0] = turned[0]
            if y == cy - GROUP:
                second[x + 1, cy - 1] = turned[GROUP - 1]

    second[1] = first[1]
    second[cx] = first[cx]

    buffers = (first, second)
    for sweep in range(SWEEPS):
        source, target = buffers[sweep % 2], buffers[(sweep + 1) % 2]

        @pl.loop(2, cx)
        def _(x):
            before, here = pieces(source, x, 0), pieces(source, x, 1)
            for y in range(1, cy - 1):
                after = pieces(source, x, y + 1)
                down, up = pieces(source, x - 1, y), pieces(source, x + 1, y)
                scale = pieces(weight, x - 1, y)
                beside = along_z(here, lane)
                for h in range(parts):
                    total = (down[h] + up[h]) + (before[h] + after[h]) + beside[h]
                    target[x, y, :, h * LANES:(h + 1) * LANES] = (
                        (1.0 - OMEGA) * here[h] + scale[h] * total
                    )
                before, here = here, after

    final = buffers[SWEEPS % 2]
    rows = pl.ds(pl.multiple_of(group * 2 * GROUP, 2 * GROUP), 2 * GROUP)

    @pl.loop(1, cx + 1)
    def _(x):
        before, here = None, pieces(final, x, 0)
        for y in range(cy):
            after = pieces(final, x, y + 1) if y + 1 < cy else None
            down, up = pieces(final, x - 1, y), pieces(final, x + 1, y)
            whole = pieces(centre, x - 1, y)
            beside = along_z(here, lane)
            for h in range(parts):
                total = (down[h] + up[h]) + beside[h]
                if before is not None:
                    total = total + before[h]
                if after is not None:
                    total = total + after[h]
                applied = whole[h] * here[h] - total
                left[x - 1, y * parts + h, rows, :] = halves(here[h])
                right[x - 1, y * parts + h, rows, :] = halves(applied)
            before, here = here, after
        for y in range(0, cy, GROUP):
            extended[:, x - 1, y:y + GROUP, :] = jnp.swapaxes(final[x, y:y + GROUP], 0, 1)

    @pl.when(group == pl.num_programs(0) - 1)
    def _():
        def add(x, total):
            one = jnp.concatenate([left[x, i] for i in range(cy * parts)], axis=1)
            other = jnp.concatenate([right[x, i] for i in range(cy * parts)], axis=1)
            return total + lax.dot_general(
                one, other, (((1,), (1,)), ((), ())), preferred_element_type=jnp.float32
            )

        size = product.shape[0]
        product[...] = lax.fori_loop(0, cx, add, jnp.zeros((size, size), jnp.float32))


def extend(basis, reaction):
    width, cx, cy, cz = basis.shape
    field = (cx + 2, cy, GROUP, cz)
    factors = pltpu.VMEM((cx, cy * cz // LANES, 2 * width, LANES), jnp.bfloat16)
    block = pl.BlockSpec((GROUP, cx, cy, cz), lambda g: (g, 0, 0, 0))
    return pl.pallas_call(
        extend_kernel,
        grid=(width // GROUP,),
        in_specs=[block, pl.BlockSpec((cx, cy, cz), lambda g: (0, 0, 0))],
        out_specs=[block, pl.BlockSpec((2 * width, 2 * width), lambda g: (0, 0))],
        out_shape=[
            jax.ShapeDtypeStruct(basis.shape, jnp.float32),
            jax.ShapeDtypeStruct((2 * width, 2 * width), jnp.float32),
        ],
        scratch_shapes=[
            pltpu.VMEM(field, jnp.float32),
            pltpu.VMEM(field, jnp.float32),
            pltpu.VMEM((cx, cy, GROUP, cz), jnp.float32),
            pltpu.VMEM((cx, cy, GROUP, cz), jnp.float32),
            factors,
            factors,
        ],
        compiler_params=pltpu.CompilerParams(vmem_limit_bytes=56 * 2**20),
        cost_estimate=pl.CostEstimate(
            flops=60 * basis.size, bytes_accessed=8 * basis.size, transcendentals=0
        ),
    )(basis, reaction)


def couple(own, other):
    width = own.shape[0]
    return -jnp.dot(
        own.reshape(width, -1),
        other.reshape(width, -1).T,
        precision=lax.Precision.HIGHEST,
        preferred_element_type=jnp.float32,
    )


def on_device(basis, reaction):
    width = basis.shape[0]
    right_face = passed_along(basis[:, 0], "gx", -1)
    upper_face = passed_along(basis[:, :, 0], "gy", -1)
    phi, product = extend(basis, reaction)
    groups = width // GROUP
    diag = product.reshape(groups, 2, GROUP, groups, 2, GROUP).sum((1, 4)).reshape(width, width)
    blocks = jnp.stack(
        [diag, couple(basis[:, -1], right_face), couple(basis[:, :, -1], upper_face)]
    )
    gathered = lax.all_gather(blocks[None], ("gx", "gy"), axis=0, tiled=True)
    columns = lax.axis_size("gy")
    plus_x = gathered[:, 1]
    plus_y = gathered[:, 2]
    minus_x = jnp.concatenate(
        [jnp.zeros((columns, width, width), jnp.float32), jnp.swapaxes(plus_x[:-columns], 1, 2)],
        axis=0,
    )
    minus_y = jnp.concatenate(
        [jnp.zeros((1, width, width), jnp.float32), jnp.swapaxes(plus_y[:-1], 1, 2)], axis=0
    )
    coarse = jnp.stack([gathered[:, 0], minus_x, plus_x, minus_y, plus_y], axis=1)
    return (phi, coarse)


def solution(mesh):
    placed = (P(None, "gx", "gy", None), P("gx", "gy", None))
    return jax.shard_map(
        on_device,
        mesh=mesh,
        in_specs=placed,
        out_specs=(P(None, "gx", "gy", None), P()),
        check_vma=False,
    )
```

time: 208 us -> 154 us (0.74)
  other arithmetic: 87.4 us -> 0.26 us
  Pallas kernels: 0 us -> 48.7 us
  matrix products: 17.1 us -> 1.11 us
    sub x5 -> x0, other arithmetic: 86.3 us -> none  [the longest x4 77 us: on_device(): phi = phi - jnp.where(inner[None], update, jnp.float32(0.0))]
    pallas_call x0 -> x1, Pallas kernels: none -> 48.7 us  [extend(): pl.pallas_call(extend_kernel, grid=(width // GROUP,), in_specs=[block, pl...]
    dot_general x1 -> x0, matrix products: 16 us -> none  [on_device(): jnp.dot(phi.reshape(width, -1), applied.reshape(width, -1).T, precision=l...]
    unnamed x11 -> x9, local copies, waits for them, and re-layouts: 4.6 us -> 4.59 us
  transfers between devices with their start and end apart: 2 -> 2, of which waited for: 0 -> 0; matrix products, arithmetic and copies ran while one was open for 51% -> 2% of each run, Pallas kernels for 0% -> 32%
where the time goes in v1:
time: 154 us; the launch traced here: 153 us
  blocking collectives  86.4 us (56%)
  Pallas kernels  48.7 us (32%)
  local copies, waits for them, and re-layouts  13.7 us (9%)
  starting transfers between devices  2.58 us (2%)
    all_gather x1, blocking collectives, on_device(): gathered = lax.all_gather(blocks[None], ('gx', 'gy'), axis=0, tiled=True)  86.4 us
    pallas_call x1, Pallas kernels, extend(): pl.pallas_call(extend_kernel, grid=(width // GROUP,), in_specs=[block, pl...  48.7 us
    slice x1, local copies, waits for them, and re-layouts, on_device(): upper_face = passed_along(basis[:, :, 0], 'gy', -1)  5.24 us
    unnamed x9, local copies, waits for them, and re-layouts  4.59 us
  transfers between devices with their start and end apart: 2, of which 0 were waited for; matrix products, arithmetic and copies ran while one was open for 2% of the time, Pallas kernels for 32%

profile of v1, /device:TPU:0, one launch (start us, length us, event | category | flops | bytes accessed | tf_op | source)
XLA Modules:
  0.0 153.5 jit_solution(16814747558122015989)
XLA Ops:
  0.6 5.2 %fusion.2 = (f32[32,16,1,256]{3,2,1,0:T(1,128)S(1)}, f32[32,16,256]{2,1,0:T(8,128)S(1)}) fusion(f32[32,16,16,256]{3,2,1,0:T(8,128)} %basis.1), kind=kLoop, calls=%fused_computation.17 | loop fusion | bytes 2097152 | tf_op jit(solution)/shard_map/slice | solution.py:176
  5.9 1.3 collective-permute-start.1
  7.2 1.3 slice_bitcast_fusion
  8.5 1.3 collective-permute-start
  9.8 0.3 copy.15
  10.1 0.3 copy.13
  10.4 48.7 %shard_map.41 = (f32[32,16,16,256]{3,2,1,0:T(8,128)}, f32[64,64]{1,0:T(8,128)}) custom-call(f32[32,16,16,256]{3,2,1,0:T(8,128)} %basis.1, f32[16,16,256]{2,1,0:T(8,128)} %reaction.1), custom_call_target="tpu_custom_call" | custom-call | flops 125829120 | bytes 16777216 | tf_op jit(solution)/shard_map/pallas_call | solution.py:139
  59.1 1.1 reshape.15
  60.2 0.2 reduce_sum.9
  60.5 0.1 stack_reshape.3
  60.6 0.0 collective-permute-done.1
  60.6 0.3 copy.16
  60.9 0.0 collective-permute-done
  60.9 0.3 copy.14
  61.2 0.5 fusion
  61.8 0.6 fusion.1
  62.4 86.4 %all-gather = f32[96,32,32]{2,1,0:T(8,128)S(1)} all-gather(f32[3,32,32]{2,1,0:T(8,128)S(1)} %pad_maximum_fusion), channel_id=2, replica_groups=mesh['gx'=8,'gy'=4] {'gx','gy'}, dimensions={0}, use_global_device_ids=true | all-gather | bytes 405504 | tf_op jit(solution)/shard_map/all_gather | solution.py:183
  148.7 0.8 slice_dynamic-update-slice_fusion.2
  149.7 0.2 copy.10
  149.9 0.8 constant_dynamic-update-slice_fusion.1
  150.7 0.8 slice_dynamic-update-slice_fusion.1
  151.6 0.2 copy.11
  151.8 0.8 constant_dynamic-update-slice_fusion
  152.6 0.8 slice_dynamic-update-slice_fusion
  (6 shorter events, 0.2 us)
Async XLA Ops:
  5.9 54.7 %collective-permute-start.1 = (f32[32,16,256]{2,1,0:T(8,128)S(1)}, f32[32,16,256]{2,1,0:T(8,128)S(1)}, u32[]{:S(2)}, u32[]{:S(2)}) collective-permute-start(f32[32,16,256]{2,1,0:T(8,128)S(1)} %bitcast.46), channel_id=1, source_target_pairs={{1,0},{2,1},{3,2},{5,4},{6,5},{7,6},{9,8},{10,9},{11,10},{13,12},{... | collective-permute-start | bytes 1572872 | tf_op jit(solution)/shard_map/ppermute | solution.py:19
  8.5 52.4 %collective-permute-start = (f32[32,16,256]{2,1,0:T(8,128)S(1)}, f32[32,16,256]{2,1,0:T(8,128)S(1)}, u32[]{:S(2)}, u32[]{:S(2)}) collective-permute-start(f32[32,16,256]{2,1,0:T(8,128)S(1)} %get-tuple-element.6), channel_id=1, source_target_pairs={{4,0},{8,4},{12,8},{16,12},{20,16},{24,20},{28,24},{5,1},{9,5},{13... | collective-permute-start | bytes 1572872 | tf_op jit(solution)/shard_map/ppermute | solution.py:19

commit v2 on v1

--- a/solution.py
+++ b/solution.py
@@ -170,29 +170,136 @@
     )
 
 
+def packed(block):
+    rows = block.shape[0] * block.shape[1] // LANES
+    return jnp.concatenate(
+        [block[i:i + rows] for i in range(0, block.shape[0], rows)], axis=1
+    )
+
+
+def unpacked(tile, width):
+    return jnp.concatenate(
+        [tile[:, i:i + width] for i in range(0, LANES, width)], axis=0
+    )
+
+
+def spread_kernel(ngx, ngy, product, plus_x, plus_y, coarse, held, send_y, recv_y, send_x, recv_x):
+    gx, gy = lax.axis_index("gx"), lax.axis_index("gy")
+    width = plus_x.shape[0]
+
+    barrier = pltpu.get_barrier_semaphore()
+    for d in range(1, ngy):
+        pl.semaphore_signal(
+            barrier, inc=1, device_id=(gx, lax.rem(gy + d, ngy)), device_id_type=pl.DeviceIdType.MESH
+        )
+    for d in range(1, ngx):
+        pl.semaphore_signal(
+            barrier, inc=1, device_id=(lax.rem(gx + d, ngx), gy), device_id_type=pl.DeviceIdType.MESH
+        )
+
+    span = 2 * GROUP
+    rows = jnp.concatenate(
+        [product[i:i + GROUP] + product[i + GROUP:i + span] for i in range(0, 2 * width, span)], axis=0
+    )
+    diag = jnp.concatenate(
+        [rows[:, i:i + GROUP] + rows[:, i + GROUP:i + span] for i in range(0, 2 * width, span)], axis=1
+    )
+    held[gx, gy, 0] = packed(diag)
+    held[gx, gy, 1] = packed(plus_x[...])
+    held[gx, gy, 2] = packed(plus_y[...])
+    for y in range(ngy):
+        coarse[y, 1] = jnp.zeros((width, width), jnp.float32)
+    coarse[0, 3] = jnp.zeros((width, width), jnp.float32)
+    pl.semaphore_wait(barrier, ngx + ngy - 2)
+
+    def over_y(owner, peer):
+        piece = held.at[gx, owner]
+        return pltpu.make_async_remote_copy(
+            src_ref=piece, dst_ref=piece, send_sem=send_y.at[peer], recv_sem=recv_y.at[owner],
+            device_id=(gx, peer), device_id_type=pl.DeviceIdType.MESH,
+        )
+
+    def over_x(row, owner, peer):
+        piece = held.at[row, owner]
+        return pltpu.make_async_remote_copy(
+            src_ref=piece, dst_ref=piece, send_sem=send_x.at[peer, owner], recv_sem=recv_x.at[row, owner],
+            device_id=(peer, gy), device_id_type=pl.DeviceIdType.MESH,
+        )
+
+    def unpack(row, owner):
+        s = row * ngy + owner
+        along_x, along_y = unpacked(held[row, owner, 1], width), unpacked(held[row, owner, 2], width)
+        coarse[s, 0] = unpacked(held[row, owner, 0], width)
+        coarse[s, 2] = along_x
+        coarse[s, 4] = along_y
+
+        @pl.when(row < ngx - 1)
+        def _():
+            coarse[s + ngy, 1] = along_x.T
+
+        @pl.when(s < ngx * ngy - 1)
+        def _():
+            coarse[s + 1, 3] = along_y.T
+
+    for d in range(1, ngy):
+        over_y(gy, lax.rem(gy + d, ngy)).start()
+    for d in range(1, ngx):
+        over_x(gx, gy, lax.rem(gx + d, ngx)).start()
+    for d in range(1, ngy):
+        owner = lax.rem(gy + d, ngy)
+        over_y(owner, owner).wait_recv()
+        for e in range(1, ngx):
+            over_x(gx, owner, lax.rem(gx + e, ngx)).start()
+
+    @pl.loop(0, ngy)
+    def _(owner):
+        unpack(gx, owner)
+
+    @pl.loop(0, ngy)
+    def _(d):
+        owner = lax.rem(gy + d, ngy)
+
+        @pl.loop(1, ngx)
+        def _(e):
+            row = lax.rem(gx + e, ngx)
+            over_x(row, owner, row).wait_recv()
+            unpack(row, owner)
+
+    for d in range(1, ngy):
+        over_y(gy, lax.rem(gy + d, ngy)).wait_send()
+    for d in range(ngy):
+        owner = lax.rem(gy + d, ngy)
+        for e in range(1, ngx):
+            over_x(gx, owner, lax.rem(gx + e, ngx)).wait_send()
+
+
+def spread(product, plus_x, plus_y):
+    ngx, ngy = lax.axis_size("gx"), lax.axis_size("gy")
+    width = plus_x.shape[0]
+    vmem = pl.BlockSpec(memory_space=pltpu.VMEM)
+    return pl.pallas_call(
+        functools.partial(spread_kernel, ngx, ngy),
+        in_specs=[vmem] * 3,
+        out_specs=vmem,
+        out_shape=jax.ShapeDtypeStruct((ngx * ngy, 5, width, width), jnp.float32),
+        scratch_shapes=[
+            pltpu.VMEM((ngx, ngy, 3, width * width // LANES, LANES), jnp.float32),
+            pltpu.SemaphoreType.DMA((ngy,)),
+            pltpu.SemaphoreType.DMA((ngy,)),
+            pltpu.SemaphoreType.DMA((ngx, ngy)),
+            pltpu.SemaphoreType.DMA((ngx, ngy)),
+        ],
+        compiler_params=pltpu.CompilerParams(collective_id=0, has_side_effects=True),
+    )(product, plus_x, plus_y)
+
+
 def on_device(basis, reaction):
-    width = basis.shape[0]
     right_face = passed_along(basis[:, 0], "gx", -1)
     upper_face = passed_along(basis[:, :, 0], "gy", -1)
     phi, product = extend(basis, reaction)
-    groups = width // GROUP
-    diag = product.reshape(groups, 2, GROUP, groups, 2, GROUP).sum((1, 4)).reshape(width, width)
-    blocks = jnp.stack(
-        [diag, couple(basis[:, -1], right_face), couple(basis[:, :, -1], upper_face)]
-    )
-    gathered = lax.all_gather(blocks[None], ("gx", "gy"), axis=0, tiled=True)
-    columns = lax.axis_size("gy")
-    plus_x = gathered[:, 1]
-    plus_y = gathered[:, 2]
-    minus_x = jnp.concatenate(
-        [jnp.zeros((columns, width, width), jnp.float32), jnp.swapaxes(plus_x[:-columns], 1, 2)],
-        axis=0,
-    )
-    minus_y = jnp.concatenate(
-        [jnp.zeros((1, width, width), jnp.float32), jnp.swapaxes(plus_y[:-1], 1, 2)], axis=0
-    )
-    coarse = jnp.stack([gathered[:, 0], minus_x, plus_x, minus_y, plus_y], axis=1)
-    return (phi, coarse)
+    plus_x = couple(basis[:, -1], right_face)
+    plus_y = couple(basis[:, :, -1], upper_face)
+    return (phi, spread(product, plus_x, plus_y))
 
 
 def solution(mesh):

time: 154 us -> 86.5 us (0.56)
  blocking collectives: 86.4 us -> 0 us
  Pallas kernels: 48.7 us -> 69.3 us
  local copies, waits for them, and re-layouts: 13.7 us -> 11.3 us
    all_gather x1 -> x0, blocking collectives: 86.4 us -> none  [on_device(): gathered = lax.all_gather(blocks[None], ('gx', 'gy'), axis=0, tiled=True)]
    pallas_call x0 -> x1, Pallas kernels: none -> 20.6 us  [spread(): pl.pallas_call(functools.partial(spread_kernel, ngx, ngy), in_specs=[vmem...]
    unnamed x9 -> x6, local copies, waits for them, and re-layouts: 4.59 us -> 4.75 us
  transfers between devices with their start and end apart: 2 -> 2, of which waited for: 0 -> 0; matrix products, arithmetic and copies ran while one was open for 2% -> 3% of each run, Pallas kernels for 32% -> 56%
where the time goes in v2:
time: 86.5 us; the launch traced here: 86.2 us
  Pallas kernels  69.3 us (80%)
  local copies, waits for them, and re-layouts  11.3 us (13%)
  starting transfers between devices  2.58 us (3%)
  matrix products  2.33 us (3%)
    pallas_call x1, Pallas kernels, extend(): pl.pallas_call(extend_kernel, grid=(width // GROUP,), in_specs=[block, pl...  48.7 us
    pallas_call x1, Pallas kernels, spread(): pl.pallas_call(functools.partial(spread_kernel, ngx, ngy), in_specs=[vmem...  20.6 us
    slice x1, local copies, waits for them, and re-layouts, on_device(): upper_face = passed_along(basis[:, :, 0], 'gy', -1)  5.28 us
    unnamed x6, local copies, waits for them, and re-layouts  4.75 us
    ppermute x2, starting transfers between devices, passed_along(): return lax.ppermute(block, axis, route)  2.58 us
    dot_general x2, matrix products, couple(): jnp.dot(own.reshape(width, -1), other.reshape(width, -1).T, precision=lax...  2.33 us
  transfers between devices with their start and end apart: 2, of which 0 were waited for; matrix products, arithmetic and copies ran while one was open for 3% of the time, Pallas kernels for 56%

profile of v2, /device:TPU:0, one launch (start us, length us, event | category | flops | bytes accessed | tf_op | source)
XLA Modules:
  0.0 86.2 jit_solution(11782828491444422131)
XLA Ops:
  0.6 5.3 %fusion = (f32[32,16,1,256]{3,2,1,0:T(1,128)S(1)}, f32[32,16,256]{2,1,0:T(8,128)S(1)}) fusion(f32[32,16,16,256]{3,2,1,0:T(8,128)} %basis.1), kind=kLoop, calls=%fused_computation.5 | loop fusion | bytes 2097152 | tf_op jit(solution)/shard_map/slice | solution.py:298
  6.0 1.3 %collective-permute-start.1 = (f32[32,16,256]{2,1,0:T(8,128)S(1)}, f32[32,16,256]{2,1,0:T(8,128)S(1)}, u32[]{:S(2)}, u32[]{:S(2)}) collective-permute-start(f32[32,16,256]{2,1,0:T(8,128)S(1)} %bitcast.24), channel_id=1, source_target_pairs={{1,0},{2,1},{3,2},{5,4},{6,5},{7,6},{9,8},{10,9},{11,10},{13,12},{... | collective-permute-start | bytes 1572872 | tf_op jit(solution)/shard_map/ppermute | solution.py:19
  7.3 1.3 %slice_bitcast_fusion = (f32[32,16,256]{2,1,0:T(8,128)S(1)}, f32[32,1,16,256]{3,2,1,0:T(8,128)S(1)}) fusion(f32[32,16,16,256]{3,2,1,0:T(8,128)} %basis.1), kind=kLoop, calls=%fused_computation.4 | loop fusion | bytes 2097152 | tf_op jit(solution)/shard_map/squeeze | solution.py:297
  8.5 1.3 %collective-permute-start = (f32[32,16,256]{2,1,0:T(8,128)S(1)}, f32[32,16,256]{2,1,0:T(8,128)S(1)}, u32[]{:S(2)}, u32[]{:S(2)}) collective-permute-start(f32[32,16,256]{2,1,0:T(8,128)S(1)} %get-tuple-element.8), channel_id=1, source_target_pairs={{4,0},{8,4},{12,8},{16,12},{20,16},{24,20},{28,24},{5,1},{9,5},{13... | collective-permute-start | bytes 1572872 | tf_op jit(solution)/shard_map/ppermute | solution.py:19
  9.8 0.3 copy.8
  10.2 0.3 copy.6
  10.5 48.7 %shard_map.41 = (f32[32,16,16,256]{3,2,1,0:T(8,128)}, f32[64,64]{1,0:T(8,128)}) custom-call(f32[32,16,16,256]{3,2,1,0:T(8,128)} %basis.1, f32[16,16,256]{2,1,0:T(8,128)} %reaction.1), custom_call_target="tpu_custom_call" | custom-call | flops 125829120 | bytes 16777216 | tf_op jit(solution)/shard_map/pallas_call | solution.py:139
  59.1 0.0 collective-permute-done.1
  59.1 0.3 copy.9
  59.4 0.0 collective-permute-done
  59.4 0.3 copy.7
  59.8 1.2 %convolution_negate_fusion.plus_y = f32[32,32]{1,0:T(8,128)} fusion(f32[32,4096]{1,0:T(8,128)S(1)} %bitcast.18, f32[32,4096]{1,0:T(8,128)S(1)} %bitcast.20), kind=kOutput, calls=%fused_computation | convolution fusion | flops 50332672 | bytes 1052672 | tf_op jit(solution)/shard_map/dot_general | solution.py:165
  60.9 1.2 %convolution_negate_fusion.1.plus_x = f32[32,32]{1,0:T(8,128)} fusion(f32[32,4096]{1,0:T(8,128)S(1)} %bitcast.19, f32[32,4096]{1,0:T(8,128)S(1)} %bitcast.21), kind=kOutput, calls=%fused_computation.1 | convolution fusion | flops 50332672 | bytes 1052672 | tf_op jit(solution)/shard_map/dot_general | solution.py:165
  62.1 20.6 %shard_map.42 = f32[32,5,32,32]{3,2,1,0:T(8,128)} custom-call(f32[64,64]{1,0:T(8,128)} %get-tuple-element.5.product, f32[32,32]{1,0:T(8,128)} %convolution_negate_fusion.1.plus_x, f32[32,32]{1,0:T(8,128)} %convolution_negate_fusion.plus_y), custom_call_target="tpu_custom_call" | custom-call | tf_op jit(solution)/shard_map/pallas_call | solution.py:280
  82.7 3.5 %copy.13 = f32[32,5,32,32]{3,2,1,0:T(8,128)} copy(f32[32,5,32,32]{3,2,1,0:T(8,128)} %shard_map.42) | data formatting | bytes 1310720
  (1 shorter events, 0.0 us)
Async XLA Ops:
  6.0 53.2 %collective-permute-start.1 = (f32[32,16,256]{2,1,0:T(8,128)S(1)}, f32[32,16,256]{2,1,0:T(8,128)S(1)}, u32[]{:S(2)}, u32[]{:S(2)}) collective-permute-start(f32[32,16,256]{2,1,0:T(8,128)S(1)} %bitcast.24), channel_id=1, source_target_pairs={{1,0},{2,1},{3,2},{5,4},{6,5},{7,6},{9,8},{10,9},{11,10},{13,12},{... | collective-permute-start | bytes 1572872 | tf_op jit(solution)/shard_map/ppermute | solution.py:19
  8.5 50.9 %collective-permute-start = (f32[32,16,256]{2,1,0:T(8,128)S(1)}, f32[32,16,256]{2,1,0:T(8,128)S(1)}, u32[]{:S(2)}, u32[]{:S(2)}) collective-permute-start(f32[32,16,256]{2,1,0:T(8,128)S(1)} %get-tuple-element.8), channel_id=1, source_target_pairs={{4,0},{8,4},{12,8},{16,12},{20,16},{24,20},{28,24},{5,1},{9,5},{13... | collective-permute-start | bytes 1572872 | tf_op jit(solution)/shard_map/ppermute | solution.py:19

commit v3 on v2

--- a/solution.py
+++ b/solution.py
@@ -41,7 +41,7 @@
     return jnp.concatenate([value, value - high], axis=0).astype(jnp.bfloat16)
 
 
-def extend_kernel(basis, reaction, extended, product, first, second, weight, centre, left, right):
+def extend_kernel(basis, reaction, extended, product, upper, first, second, weight, centre, left, right):
     _, cx, cy, cz = basis.shape
     parts = cz // LANES
     group = pl.program_id(0)
@@ -79,7 +79,7 @@
     for sweep in range(SWEEPS):
         source, target = buffers[sweep % 2], buffers[(sweep + 1) % 2]
 
-        @pl.loop(2, cx)
+        @pl.loop(2, cx, unroll=2)
         def _(x):
             before, here = pieces(source, x, 0), pieces(source, x, 1)
             for y in range(1, cy - 1):
@@ -118,6 +118,9 @@
         for y in range(0, cy, GROUP):
             extended[:, x - 1, y:y + GROUP, :] = jnp.swapaxes(final[x, y:y + GROUP], 0, 1)
 
+    for x in range(0, cx, GROUP):
+        upper[:, x:x + GROUP, :] = jnp.swapaxes(final[x + 1:x + 1 + GROUP, cy - 1], 0, 1)
+
     @pl.when(group == pl.num_programs(0) - 1)
     def _():
         def add(x, total):
@@ -140,10 +143,15 @@
         extend_kernel,
         grid=(width // GROUP,),
         in_specs=[block, pl.BlockSpec((cx, cy, cz), lambda g: (0, 0, 0))],
-        out_specs=[block, pl.BlockSpec((2 * width, 2 * width), lambda g: (0, 0))],
+        out_specs=[
+            block,
+            pl.BlockSpec((2 * width, 2 * width), lambda g: (0, 0)),
+            pl.BlockSpec((GROUP, cx, cz), lambda g: (g, 0, 0)),
+        ],
         out_shape=[
             jax.ShapeDtypeStruct(basis.shape, jnp.float32),
             jax.ShapeDtypeStruct((2 * width, 2 * width), jnp.float32),
+            jax.ShapeDtypeStruct((width, cx, cz), jnp.float32),
         ],
         scratch_shapes=[
             pltpu.VMEM(field, jnp.float32),
@@ -160,6 +168,21 @@
     )(basis, reaction)
 
 
+def face_kernel(basis, face):
+    face[...] = basis[:, :, 0, :]
+
+
+def lower_face(basis):
+    width, cx, _, cz = basis.shape
+    return pl.pallas_call(
+        face_kernel,
+        grid=(width // GROUP,),
+        in_specs=[pl.BlockSpec((GROUP, cx, GROUP, cz), lambda g: (g, 0, 0, 0))],
+        out_specs=pl.BlockSpec((GROUP, cx, cz), lambda g: (g, 0, 0)),
+        out_shape=jax.ShapeDtypeStruct((width, cx, cz), jnp.float32),
+    )(basis)
+
+
 def couple(own, other):
     width = own.shape[0]
     return -jnp.dot(
@@ -219,10 +242,10 @@
             device_id=(gx, peer), device_id_type=pl.DeviceIdType.MESH,
         )
 
-    def over_x(row, owner, peer):
-        piece = held.at[row, owner]
+    def over_x(row, peer):
+        piece = held.at[row]
         return pltpu.make_async_remote_copy(
-            src_ref=piece, dst_ref=piece, send_sem=send_x.at[peer, owner], recv_sem=recv_x.at[row, owner],
+            src_ref=piece, dst_ref=piece, send_sem=send_x.at[peer], recv_sem=recv_x.at[row],
             device_id=(peer, gy), device_id_type=pl.DeviceIdType.MESH,
         )
 
@@ -243,34 +266,29 @@
 
     for d in range(1, ngy):
         over_y(gy, lax.rem(gy + d, ngy)).start()
-    for d in range(1, ngx):
-        over_x(gx, gy, lax.rem(gx + d, ngx)).start()
     for d in range(1, ngy):
         owner = lax.rem(gy + d, ngy)
         over_y(owner, owner).wait_recv()
-        for e in range(1, ngx):
-            over_x(gx, owner, lax.rem(gx + e, ngx)).start()
+    for e in range(1, ngx):
+        over_x(gx, lax.rem(gx + e, ngx)).start()
 
     @pl.loop(0, ngy)
     def _(owner):
         unpack(gx, owner)
 
-    @pl.loop(0, ngy)
-    def _(d):
-        owner = lax.rem(gy + d, ngy)
-
-        @pl.loop(1, ngx)
-        def _(e):
-            row = lax.rem(gx + e, ngx)
-            over_x(row, owner, row).wait_recv()
+    @pl.loop(1, ngx)
+    def _(e):
+        row = lax.rem(gx + e, ngx)
+        over_x(row, row).wait_recv()
+
+        @pl.loop(0, ngy)
+        def _(owner):
             unpack(row, owner)
 
     for d in range(1, ngy):
         over_y(gy, lax.rem(gy + d, ngy)).wait_send()
-    for d in range(ngy):
-        owner = lax.rem(gy + d, ngy)
-        for e in range(1, ngx):
-            over_x(gx, owner, lax.rem(gx + e, ngx)).wait_send()
+    for e in range(1, ngx):
+        over_x(gx, lax.rem(gx + e, ngx)).wait_send()
 
 
 def spread(product, plus_x, plus_y):
@@ -286,8 +304,8 @@
             pltpu.VMEM((ngx, ngy, 3, width * width // LANES, LANES), jnp.float32),
             pltpu.SemaphoreType.DMA((ngy,)),
             pltpu.SemaphoreType.DMA((ngy,)),
-            pltpu.SemaphoreType.DMA((ngx, ngy)),
-            pltpu.SemaphoreType.DMA((ngx, ngy)),
+            pltpu.SemaphoreType.DMA((ngx,)),
+            pltpu.SemaphoreType.DMA((ngx,)),
         ],
         compiler_params=pltpu.CompilerParams(collective_id=0, has_side_effects=True),
     )(product, plus_x, plus_y)
@@ -295,10 +313,10 @@
 
 def on_device(basis, reaction):
     right_face = passed_along(basis[:, 0], "gx", -1)
-    upper_face = passed_along(basis[:, :, 0], "gy", -1)
-    phi, product = extend(basis, reaction)
+    upper_face = passed_along(lower_face(basis), "gy", -1)
+    phi, product, upper = extend(basis, reaction)
     plus_x = couple(basis[:, -1], right_face)
-    plus_y = couple(basis[:, :, -1], upper_face)
+    plus_y = couple(upper, upper_face)
     return (phi, spread(product, plus_x, plus_y))
 
 

time: 86.5 us -> 81.8 us (0.946)
  local copies, waits for them, and re-layouts: 11.3 us -> 5.38 us
  matrix products: 2.33 us -> 3.91 us
  Pallas kernels: 69.3 us -> 68.2 us
    pallas_call x1, Pallas kernels: 48.7 us -> 40.8 us  [extend(): pl.pallas_call(extend_kernel, grid=(width // GROUP,), in_specs=[block, pl...]
    slice x1 -> x0, local copies, waits for them, and re-layouts: 5.28 us -> none  [on_device(): upper_face = passed_along(basis[:, :, 0], 'gy', -1)]
    pallas_call x0 -> x1, Pallas kernels: none -> 3.92 us  [lower_face(): pl.pallas_call(face_kernel, grid=(width // GROUP,), in_specs=[pl.BlockSpe...]
    pallas_call x1, Pallas kernels: 20.6 us -> 23.5 us  [spread(): pl.pallas_call(functools.partial(spread_kernel, ngx, ngy), in_specs=[vmem...]
    dot_general x2, matrix products: 2.33 us -> 3.91 us  [couple(): jnp.dot(own.reshape(width, -1), other.reshape(width, -1).T, precision=lax...]
    unnamed x6 -> x3, local copies, waits for them, and re-layouts: 4.75 us -> 4.1 us
  transfers between devices with their start and end apart: 2 -> 2, of which waited for: 0 -> 0; matrix products, arithmetic and copies ran while one was open for 3% -> 2% of each run, Pallas kernels for 56% -> 55%
where the time goes in v3:
time: 81.8 us; the launch traced here: 80.7 us
  Pallas kernels  68.2 us (83%)
  local copies, waits for them, and re-layouts  5.38 us (7%)
  matrix products  3.91 us (5%)
  starting transfers between devices  2.57 us (3%)
    pallas_call x1, Pallas kernels, extend(): pl.pallas_call(extend_kernel, grid=(width // GROUP,), in_specs=[block, pl...  40.8 us
    pallas_call x1, Pallas kernels, spread(): pl.pallas_call(functools.partial(spread_kernel, ngx, ngy), in_specs=[vmem...  23.5 us
    unnamed x3, local copies, waits for them, and re-layouts  4.1 us
    pallas_call x1, Pallas kernels, lower_face(): pl.pallas_call(face_kernel, grid=(width // GROUP,), in_specs=[pl.BlockSpe...  3.92 us
    dot_general x2, matrix products, couple(): jnp.dot(own.reshape(width, -1), other.reshape(width, -1).T, precision=lax...  3.91 us
    ppermute x2, starting transfers between devices, passed_along(): return lax.ppermute(block, axis, route)  2.57 us
  transfers between devices with their start and end apart: 2, of which 0 were waited for; matrix products, arithmetic and copies ran while one was open for 2% of the time, Pallas kernels for 55%

profile of v3, /device:TPU:0, one launch (start us, length us, event | category | flops | bytes accessed | tf_op | source)
XLA Modules:
  0.0 80.7 jit_solution(15924146764926822900)
XLA Ops:
  0.6 1.3 %slice_bitcast_fusion = (f32[32,16,256]{2,1,0:T(8,128)S(1)}, f32[32,1,16,256]{3,2,1,0:T(8,128)S(1)}) fusion(f32[32,16,16,256]{3,2,1,0:T(8,128)} %basis.3), kind=kLoop, calls=%fused_computation.5 | loop fusion | bytes 2097152 | tf_op jit(solution)/shard_map/squeeze | solution.py:315
  1.9 1.3 %collective-permute-start = (f32[32,16,256]{2,1,0:T(8,128)S(1)}, f32[32,16,256]{2,1,0:T(8,128)S(1)}, u32[]{:S(2)}, u32[]{:S(2)}) collective-permute-start(f32[32,16,256]{2,1,0:T(8,128)S(1)} %get-tuple-element.8), channel_id=1, source_target_pairs={{4,0},{8,4},{12,8},{16,12},{20,16},{24,20},{28,24},{5,1},{9,5},{13... | collective-permute-start | bytes 1572872 | tf_op jit(solution)/shard_map/ppermute | solution.py:19
  3.2 3.9 %shard_map.42 = f32[32,16,256]{2,1,0:T(8,128)} custom-call(f32[32,16,16,256]{3,2,1,0:T(8,128)} %basis.3), custom_call_target="tpu_custom_call" | custom-call | tf_op jit(solution)/shard_map/pallas_call | solution.py:177
  7.1 1.3 %collective-permute-start.1 = (f32[32,16,256]{2,1,0:T(8,128)}, f32[32,16,256]{2,1,0:T(8,128)S(1)}, u32[]{:S(2)}, u32[]{:S(2)}) collective-permute-start(f32[32,16,256]{2,1,0:T(8,128)} %shard_map.42), channel_id=1, source_target_pairs={{1,0},{2,1},{3,2},{5,4},{6,5},{7,6},{9,8},{10,9},{11,10},{13,12},{... | collective-permute-start | bytes 1572872 | tf_op jit(solution)/shard_map/ppermute | solution.py:19
  8.4 0.3 copy.6
  8.7 40.8 %shard_map.41 = (f32[32,16,16,256]{3,2,1,0:T(8,128)}, f32[64,64]{1,0:T(8,128)}, f32[32,16,256]{2,1,0:T(8,128)}) custom-call(f32[32,16,16,256]{3,2,1,0:T(8,128)} %basis.3, f32[16,16,256]{2,1,0:T(8,128)} %reaction.1), custom_call_target="tpu_custom_call" | custom-call | flops 125829120 | bytes 16777216 | tf_op jit(solution)/shard_map/pallas_call | solution.py:142
  49.5 0.0 collective-permute-done
  49.5 0.3 copy.7
  49.9 1.2 %convolution_negate_fusion.plus_x = f32[32,32]{1,0:T(8,128)} fusion(f32[32,4096]{1,0:T(8,128)S(1)} %bitcast.13, f32[32,4096]{1,0:T(8,128)S(1)} %bitcast.14), kind=kOutput, calls=%fused_computation.2 | convolution fusion | flops 50332672 | bytes 1052672 | tf_op jit(solution)/shard_map/dot_general | solution.py:188
  51.0 0.0 collective-permute-done.1
  51.0 2.7 %fusion.plus_y = f32[32,32]{1,0:T(8,128)} fusion(f32[32,16,256]{2,1,0:T(8,128)S(1)} %collective-permute-done.1, f32[32,16,256]{2,1,0:T(8,128)} %get-tuple-element.7), kind=kOutput, calls=%fused_computation.1 | convolution fusion | flops 50332672 | bytes 1052672 | tf_op jit(solution)/shard_map/dot_general | solution.py:188
  53.8 23.5 %shard_map.43 = f32[32,5,32,32]{3,2,1,0:T(8,128)} custom-call(f32[64,64]{1,0:T(8,128)} %get-tuple-element.6.product, f32[32,32]{1,0:T(8,128)} %convolution_negate_fusion.plus_x, f32[32,32]{1,0:T(8,128)} %fusion.plus_y), custom_call_target="tpu_custom_call" | custom-call | tf_op jit(solution)/shard_map/pallas_call | solution.py:298
  77.2 3.5 %copy.13 = f32[32,5,32,32]{3,2,1,0:T(8,128)} copy(f32[32,5,32,32]{3,2,1,0:T(8,128)} %shard_map.43) | data formatting | bytes 1310720
Async XLA Ops:
  1.9 47.6 %collective-permute-start = (f32[32,16,256]{2,1,0:T(8,128)S(1)}, f32[32,16,256]{2,1,0:T(8,128)S(1)}, u32[]{:S(2)}, u32[]{:S(2)}) collective-permute-start(f32[32,16,256]{2,1,0:T(8,128)S(1)} %get-tuple-element.8), channel_id=1, source_target_pairs={{4,0},{8,4},{12,8},{16,12},{20,16},{24,20},{28,24},{5,1},{9,5},{13... | collective-permute-start | bytes 1572872 | tf_op jit(solution)/shard_map/ppermute | solution.py:19
  7.1 43.9 %collective-permute-start.1 = (f32[32,16,256]{2,1,0:T(8,128)}, f32[32,16,256]{2,1,0:T(8,128)S(1)}, u32[]{:S(2)}, u32[]{:S(2)}) collective-permute-start(f32[32,16,256]{2,1,0:T(8,128)} %shard_map.42), channel_id=1, source_target_pairs={{1,0},{2,1},{3,2},{5,4},{6,5},{7,6},{9,8},{10,9},{11,10},{13,12},{... | collective-permute-start | bytes 1572872 | tf_op jit(solution)/shard_map/ppermute | solution.py:19

commit v4 on v2

--- a/solution.py
+++ b/solution.py
@@ -41,7 +41,7 @@
     return jnp.concatenate([value, value - high], axis=0).astype(jnp.bfloat16)
 
 
-def extend_kernel(basis, reaction, extended, product, first, second, weight, centre, left, right):
+def extend_kernel(basis, reaction, extended, product, upper, first, second, weight, centre, left, right):
     _, cx, cy, cz = basis.shape
     parts = cz // LANES
     group = pl.program_id(0)
@@ -62,7 +62,7 @@
                 centre[x, y] = jnp.broadcast_to(whole[y:y + 1], (GROUP, cz))
                 weight[x, y] = jnp.broadcast_to(scaled[y:y + 1], (GROUP, cz))
 
-    @pl.loop(0, cx)
+    @pl.loop(0, cx, unroll=2)
     def _(x):
         for y in range(0, cy, GROUP):
             turned = jnp.swapaxes(basis[:, x, y:y + GROUP, :], 0, 1)
@@ -79,7 +79,7 @@
     for sweep in range(SWEEPS):
         source, target = buffers[sweep % 2], buffers[(sweep + 1) % 2]
 
-        @pl.loop(2, cx)
+        @pl.loop(2, cx, unroll=7)
         def _(x):
             before, here = pieces(source, x, 0), pieces(source, x, 1)
             for y in range(1, cy - 1):
@@ -97,7 +97,7 @@
     final = buffers[SWEEPS % 2]
     rows = pl.ds(pl.multiple_of(group * 2 * GROUP, 2 * GROUP), 2 * GROUP)
 
-    @pl.loop(1, cx + 1)
+    @pl.loop(1, cx + 1, unroll=2)
     def _(x):
         before, here = None, pieces(final, x, 0)
         for y in range(cy):
@@ -118,6 +118,9 @@
         for y in range(0, cy, GROUP):
             extended[:, x - 1, y:y + GROUP, :] = jnp.swapaxes(final[x, y:y + GROUP], 0, 1)
 
+    for x in range(0, cx, GROUP):
+        upper[:, x:x + GROUP, :] = jnp.swapaxes(final[x + 1:x + 1 + GROUP, cy - 1], 0, 1)
+
     @pl.when(group == pl.num_programs(0) - 1)
     def _():
         def add(x, total):
@@ -140,10 +143,15 @@
         extend_kernel,
         grid=(width // GROUP,),
         in_specs=[block, pl.BlockSpec((cx, cy, cz), lambda g: (0, 0, 0))],
-        out_specs=[block, pl.BlockSpec((2 * width, 2 * width), lambda g: (0, 0))],
+        out_specs=[
+            block,
+            pl.BlockSpec((2 * width, 2 * width), lambda g: (0, 0)),
+            pl.BlockSpec((GROUP, cx, cz), lambda g: (g, 0, 0)),
+        ],
         out_shape=[
             jax.ShapeDtypeStruct(basis.shape, jnp.float32),
             jax.ShapeDtypeStruct((2 * width, 2 * width), jnp.float32),
+            jax.ShapeDtypeStruct((width, cx, cz), jnp.float32),
         ],
         scratch_shapes=[
             pltpu.VMEM(field, jnp.float32),
@@ -158,6 +166,21 @@
             flops=60 * basis.size, bytes_accessed=8 * basis.size, transcendentals=0
         ),
     )(basis, reaction)
+
+
+def face_kernel(basis, face):
+    face[...] = basis[:, :, 0, :]
+
+
+def lower_face(basis):
+    width, cx, _, cz = basis.shape
+    return pl.pallas_call(
+        face_kernel,
+        grid=(width // GROUP,),
+        in_specs=[pl.BlockSpec((GROUP, cx, GROUP, cz), lambda g: (g, 0, 0, 0))],
+        out_specs=pl.BlockSpec((GROUP, cx, cz), lambda g: (g, 0, 0)),
+        out_shape=jax.ShapeDtypeStruct((width, cx, cz), jnp.float32),
+    )(basis)
 
 
 def couple(own, other):
@@ -295,10 +318,10 @@
 
 def on_device(basis, reaction):
     right_face = passed_along(basis[:, 0], "gx", -1)
-    upper_face = passed_along(basis[:, :, 0], "gy", -1)
-    phi, product = extend(basis, reaction)
+    upper_face = passed_along(lower_face(basis), "gy", -1)
+    phi, product, upper = extend(basis, reaction)
     plus_x = couple(basis[:, -1], right_face)
-    plus_y = couple(basis[:, :, -1], upper_face)
+    plus_y = couple(upper, upper_face)
     return (phi, spread(product, plus_x, plus_y))
 
 

time: 86.5 us -> 69.7 us (0.81)
  Pallas kernels: 69.3 us -> 56.8 us
  local copies, waits for them, and re-layouts: 11.3 us -> 5.38 us
  matrix products: 2.33 us -> 3.91 us
    pallas_call x1, Pallas kernels: 48.7 us -> 32.4 us  [extend(): pl.pallas_call(extend_kernel, grid=(width // GROUP,), in_specs=[block, pl...]
    slice x1 -> x0, local copies, waits for them, and re-layouts: 5.28 us -> none  [on_device(): upper_face = passed_along(basis[:, :, 0], 'gy', -1)]
    pallas_call x0 -> x1, Pallas kernels: none -> 3.92 us  [lower_face(): pl.pallas_call(face_kernel, grid=(width // GROUP,), in_specs=[pl.BlockSpe...]
    dot_general x2, matrix products: 2.33 us -> 3.91 us  [couple(): jnp.dot(own.reshape(width, -1), other.reshape(width, -1).T, precision=lax...]
    unnamed x6 -> x3, local copies, waits for them, and re-layouts: 4.75 us -> 4.1 us
  transfers between devices with their start and end apart: 2 -> 2, of which waited for: 0 -> 0; matrix products, arithmetic and copies ran while one was open for 3% -> 3% of each run, Pallas kernels for 56% -> 52%
where the time goes in v4:
time: 69.7 us; the launch traced here: 69.3 us
  Pallas kernels  56.8 us (81%)
  local copies, waits for them, and re-layouts  5.38 us (8%)
  matrix products  3.91 us (6%)
  starting transfers between devices  2.57 us (4%)
    pallas_call x1, Pallas kernels, extend(): pl.pallas_call(extend_kernel, grid=(width // GROUP,), in_specs=[block, pl...  32.4 us
    pallas_call x1, Pallas kernels, spread(): pl.pallas_call(functools.partial(spread_kernel, ngx, ngy), in_specs=[vmem...  20.5 us
    unnamed x3, local copies, waits for them, and re-layouts  4.1 us
    pallas_call x1, Pallas kernels, lower_face(): pl.pallas_call(face_kernel, grid=(width // GROUP,), in_specs=[pl.BlockSpe...  3.92 us
    dot_general x2, matrix products, couple(): jnp.dot(own.reshape(width, -1), other.reshape(width, -1).T, precision=lax...  3.91 us
    ppermute x2, starting transfers between devices, passed_along(): return lax.ppermute(block, axis, route)  2.57 us
  transfers between devices with their start and end apart: 2, of which 0 were waited for; matrix products, arithmetic and copies ran while one was open for 3% of the time, Pallas kernels for 52%

profile of v4, /device:TPU:0, one launch (start us, length us, event | category | flops | bytes accessed | tf_op | source)
XLA Modules:
  0.0 69.3 jit_solution(13807315031728467791)
XLA Ops:
  0.6 1.3 %slice_bitcast_fusion = (f32[32,16,256]{2,1,0:T(8,128)S(1)}, f32[32,1,16,256]{3,2,1,0:T(8,128)S(1)}) fusion(f32[32,16,16,256]{3,2,1,0:T(8,128)} %basis.3), kind=kLoop, calls=%fused_computation.5 | loop fusion | bytes 2097152 | tf_op jit(solution)/shard_map/squeeze | solution.py:320
  1.9 1.3 %collective-permute-start = (f32[32,16,256]{2,1,0:T(8,128)S(1)}, f32[32,16,256]{2,1,0:T(8,128)S(1)}, u32[]{:S(2)}, u32[]{:S(2)}) collective-permute-start(f32[32,16,256]{2,1,0:T(8,128)S(1)} %get-tuple-element.8), channel_id=1, source_target_pairs={{4,0},{8,4},{12,8},{16,12},{20,16},{24,20},{28,24},{5,1},{9,5},{13... | collective-permute-start | bytes 1572872 | tf_op jit(solution)/shard_map/ppermute | solution.py:19
  3.2 3.9 %shard_map.42 = f32[32,16,256]{2,1,0:T(8,128)} custom-call(f32[32,16,16,256]{3,2,1,0:T(8,128)} %basis.3), custom_call_target="tpu_custom_call" | custom-call | tf_op jit(solution)/shard_map/pallas_call | solution.py:177
  7.1 1.3 %collective-permute-start.1 = (f32[32,16,256]{2,1,0:T(8,128)}, f32[32,16,256]{2,1,0:T(8,128)S(1)}, u32[]{:S(2)}, u32[]{:S(2)}) collective-permute-start(f32[32,16,256]{2,1,0:T(8,128)} %shard_map.42), channel_id=1, source_target_pairs={{1,0},{2,1},{3,2},{5,4},{6,5},{7,6},{9,8},{10,9},{11,10},{13,12},{... | collective-permute-start | bytes 1572872 | tf_op jit(solution)/shard_map/ppermute | solution.py:19
  8.4 0.3 copy.6
  8.7 32.4 %shard_map.41 = (f32[32,16,16,256]{3,2,1,0:T(8,128)}, f32[64,64]{1,0:T(8,128)}, f32[32,16,256]{2,1,0:T(8,128)}) custom-call(f32[32,16,16,256]{3,2,1,0:T(8,128)} %basis.3, f32[16,16,256]{2,1,0:T(8,128)} %reaction.1), custom_call_target="tpu_custom_call" | custom-call | flops 125829120 | bytes 16777216 | tf_op jit(solution)/shard_map/pallas_call | solution.py:142
  41.1 0.0 collective-permute-done
  41.1 0.3 copy.7
  41.4 1.2 %convolution_negate_fusion.plus_x = f32[32,32]{1,0:T(8,128)} fusion(f32[32,4096]{1,0:T(8,128)S(1)} %bitcast.13, f32[32,4096]{1,0:T(8,128)S(1)} %bitcast.14), kind=kOutput, calls=%fused_computation.2 | convolution fusion | flops 50332672 | bytes 1052672 | tf_op jit(solution)/shard_map/dot_general | solution.py:188
  42.6 0.0 collective-permute-done.1
  42.6 2.7 %fusion.plus_y = f32[32,32]{1,0:T(8,128)} fusion(f32[32,16,256]{2,1,0:T(8,128)S(1)} %collective-permute-done.1, f32[32,16,256]{2,1,0:T(8,128)} %get-tuple-element.7), kind=kOutput, calls=%fused_computation.1 | convolution fusion | flops 50332672 | bytes 1052672 | tf_op jit(solution)/shard_map/dot_general | solution.py:188
  45.3 20.5 %shard_map.43 = f32[32,5,32,32]{3,2,1,0:T(8,128)} custom-call(f32[64,64]{1,0:T(8,128)} %get-tuple-element.6.product, f32[32,32]{1,0:T(8,128)} %convolution_negate_fusion.plus_x, f32[32,32]{1,0:T(8,128)} %fusion.plus_y), custom_call_target="tpu_custom_call" | custom-call | tf_op jit(solution)/shard_map/pallas_call | solution.py:303
  65.8 3.5 %copy.13 = f32[32,5,32,32]{3,2,1,0:T(8,128)} copy(f32[32,5,32,32]{3,2,1,0:T(8,128)} %shard_map.43) | data formatting | bytes 1310720
Async XLA Ops:
  1.9 39.2 %collective-permute-start = (f32[32,16,256]{2,1,0:T(8,128)S(1)}, f32[32,16,256]{2,1,0:T(8,128)S(1)}, u32[]{:S(2)}, u32[]{:S(2)}) collective-permute-start(f32[32,16,256]{2,1,0:T(8,128)S(1)} %get-tuple-element.8), channel_id=1, source_target_pairs={{4,0},{8,4},{12,8},{16,12},{20,16},{24,20},{28,24},{5,1},{9,5},{13... | collective-permute-start | bytes 1572872 | tf_op jit(solution)/shard_map/ppermute | solution.py:19
  7.1 35.5 %collective-permute-start.1 = (f32[32,16,256]{2,1,0:T(8,128)}, f32[32,16,256]{2,1,0:T(8,128)S(1)}, u32[]{:S(2)}, u32[]{:S(2)}) collective-permute-start(f32[32,16,256]{2,1,0:T(8,128)} %shard_map.42), channel_id=1, source_target_pairs={{1,0},{2,1},{3,2},{5,4},{6,5},{7,6},{9,8},{10,9},{11,10},{13,12},{... | collective-permute-start | bytes 1572872 | tf_op jit(solution)/shard_map/ppermute | solution.py:19
